TPU v7x, 512 devices: a whole 4x8x8 slice. The times are simulated.
512 devices in a mesh: group: 2 (over z_lo), dp: 8 (over y), tensor: 32 (over z_hi, x, core).
Axes of the slice: x: 4, y: 8, z: 8 (z_hi: 4, z_lo: 2; z = z_hi * 2 + z_lo), core: 2. Of those that a mesh axis runs over, the one named last changes fastest.
Arguments:
- image_feats: bfloat16 [2048, 7680], P('tensor', ('group', 'dp')), may hold values from -6 to 6
- proj_weight: bfloat16 [7680, 8192], P(('group', 'dp'), 'tensor'), may hold values from -0.0625 to 0.0625
- proj_bias: bfloat16 [8192], P('tensor'), may hold values from -3 to 3
- kv_weight: bfloat16 [8192, 2048], P('tensor'), may hold values from -0.0625 to 0.0625
- queries: bfloat16 [4096, 8192], P(('group', 'dp'), 'tensor'), may hold values from -14 to 14
- out_grad: bfloat16 [4096, 8192], P(('group', 'dp'), 'tensor'), may hold values from -6 to 6
- image_sample: int32 [16, 128], P(('group', 'dp')), may hold values from 0 to 3, as said below
- text_sample: int32 [16, 256], P(('group', 'dp')), may hold values from 0 to 3, as said below
Outputs:
- attended: bfloat16 [4096, 8192], P(('group', 'dp'), 'tensor')
- d_queries: bfloat16 [4096, 8192], P(('group', 'dp'), 'tensor')
- d_proj_weight: bfloat16 [7680, 8192], P(('group', 'dp'), 'tensor')
- d_proj_bias: float32 [8192], P('tensor')
- d_kv_weight: bfloat16 [8192, 2048], P('tensor', ('group', 'dp'))
Inputs may be any that keep to these rules, and one draw needn't show every extreme that they name: `image_sample`: within each row (one data shard) the sample numbers never fall and every number from 0 to 3 occurs. `text_sample`: within each row (one data shard) the sample numbers never fall and every number from 0 to 3 occurs.
All inputs are finite; a program needn't handle non-finite values.
Results may differ from a plain program's by a relative error of at most 0.04.
Values may be sent and summed in bfloat16 or wider, within the bound.
A program may use at most 64 MiB of HBM per device.

v0:
```python
import jax
import jax.numpy as jnp
from jax import lax
from jax.sharding import PartitionSpec as P

H = 64
KVH = 8
HD = 128


def joined_along(tiles, dim):
    lengths = list(tiles.shape[1:])
    lengths[dim] *= tiles.shape[0]
    return jnp.moveaxis(tiles, 0, dim).reshape(lengths)


def from_everyone(shard, axis):
    devices = lax.axis_size(axis)
    return lax.all_to_all(
        jnp.broadcast_to(shard[None], (devices, *shard.shape)), axis, 0, 0, tiled=True
    )


def gathered_copies(shard, axis, dim):
    return joined_along(from_everyone(shard, axis), dim)


def split_up(shard, dim, devices):
    lengths = shard.shape
    tiles = shard.reshape(*lengths[:dim], devices, lengths[dim] // devices, *lengths[dim + 1 :])
    return jnp.moveaxis(tiles, dim, 0)


def sent_and_summed(shard, axis, dim):
    devices = lax.axis_size(axis)
    tiles = lax.all_to_all(split_up(shard, dim, devices), axis, 0, 0, tiled=True)
    return jnp.sum(tiles.astype(jnp.float32), axis=0)


def sum_at_owner(shard, axis, dim):
    devices = lax.axis_size(axis)
    tiles = lax.all_to_all(split_up(shard, dim, devices), axis, 0, 0, tiled=True)
    return jnp.sum(tiles, axis=0)


def from_partner(shard, axis, distance):
    return lax.ppermute(shard, axis, [(i, i ^ 1 << distance) for i in range(lax.axis_size(axis))])


def shards(
    image_feats, proj_weight, proj_bias, kv_weight, queries, out_grad, image_sample, text_sample
):
    gathered = gathered_copies(image_feats, "tensor", 0)
    rows = gathered
    summed = sent_and_summed(
        jnp.dot(rows, proj_weight, preferred_element_type=jnp.float32).astype(jnp.bfloat16),
        ("group", "dp"),
        0,
    )
    projected = (summed + proj_bias.astype(jnp.float32)[None, :]).astype(jnp.bfloat16)
    kv_term = jnp.dot(projected, kv_weight, preferred_element_type=jnp.float32)
    kv_part = sum_at_owner(kv_term, "tensor", 1).astype(jnp.bfloat16)
    kv_all = gathered_copies(kv_part, "tensor", 1)
    local_heads = queries.shape[1] // HD
    shared = H // KVH
    half = kv_all.shape[1] // 2
    key_head = lax.axis_index("tensor") * local_heads // shared
    key_start = key_head * HD
    keys = lax.dynamic_slice_in_dim(kv_all, key_start, HD, 1)
    values = lax.dynamic_slice_in_dim(kv_all, key_start + half, HD, 1)
    scale = HD ** (-0.5)
    q_rows = queries.reshape(queries.shape[0], local_heads, HD)
    grads = out_grad.reshape(out_grad.shape[0], local_heads, HD)
    scores = jnp.einsum("thd,id->hti", q_rows, keys, preferred_element_type=jnp.float32) * scale
    allowed = text_sample[0][:, None] == image_sample[0][None, :]
    scores = jnp.where(allowed[None], scores, jnp.float32(-1e30))
    peak = jnp.max(scores, axis=-1, keepdims=True)
    expo = jnp.exp(scores - peak)
    probs = expo / jnp.sum(expo, axis=-1, keepdims=True)
    probs_b = probs.astype(jnp.bfloat16)
    attended = jnp.einsum(
        "hti,id->thd", probs_b, values, preferred_element_type=jnp.float32
    ).astype(jnp.bfloat16)
    dprobs = jnp.einsum("thd,id->hti", grads, values, preferred_element_type=jnp.float32)
    delta = jnp.sum(probs * dprobs, axis=-1, keepdims=True)
    dscores = (probs * (dprobs - delta) * scale).astype(jnp.bfloat16)
    d_rows = jnp.einsum("hti,id->thd", dscores, keys, preferred_element_type=jnp.float32).astype(
        jnp.bfloat16
    )
    d_keys = jnp.einsum("hti,thd->id", dscores, q_rows, preferred_element_type=jnp.float32)
    d_values = jnp.einsum("hti,thd->id", probs_b, grads, preferred_element_type=jnp.float32)
    image_count = kv_term.shape[0]
    members = shared // local_heads
    stacked = jnp.concatenate([d_keys, d_values], axis=1)
    for level in range(members.bit_length() - 1):
        stacked = stacked + from_partner(stacked, "tensor", level)
    width = stacked.shape[1] // members
    member = lax.axis_index("tensor") % members
    mine = lax.dynamic_slice_in_dim(stacked, member * width, width, 1).astype(jnp.bfloat16)
    collected = gathered_copies(mine, "tensor", 1)
    heads_total = collected.shape[1] // (2 * HD)
    dkv = (
        collected.reshape(image_count, heads_total, 2, HD)
        .transpose(0, 2, 1, 3)
        .reshape(image_count, 2 * heads_total * HD)
    )
    d_projected = lax.dot_general(
        dkv, kv_weight, (((1,), (1,)), ((), ())), preferred_element_type=jnp.float32
    ).astype(jnp.bfloat16)
    kv_grad_term = lax.dot_general(
        projected, dkv, (((0,), (0,)), ((), ())), preferred_element_type=jnp.float32
    )
    d_kv_weight = sent_and_summed(kv_grad_term.astype(jnp.bfloat16), ("group", "dp"), 1).astype(
        jnp.bfloat16
    )
    piece = gathered_copies(d_projected, ("group", "dp"), 0)
    rows = gathered
    weight_grad = lax.dot_general(
        rows, piece, (((0,), (0,)), ((), ())), preferred_element_type=jnp.float32
    )
    bias_grad = jnp.sum(piece.astype(jnp.float32), axis=0)
    weight_grad, bias_grad = (weight_grad, bias_grad)
    attended = attended.reshape(queries.shape)
    d_queries = d_rows.reshape(queries.shape)
    return (attended, d_queries, weight_grad.astype(jnp.bfloat16), bias_grad, d_kv_weight)


def solution(mesh):
    in_specs = (
        P("tensor", ("group", "dp")),
        P(("group", "dp"), "tensor"),
        P("tensor"),
        P("tensor", None),
        P(("group", "dp"), "tensor"),
        P(("group", "dp"), "tensor"),
        P(("group", "dp"), None),
        P(("group", "dp"), None),
    )
    out_specs = (
        P(("group", "dp"), "tensor"),
        P(("group", "dp"), "tensor"),
        P(("group", "dp"), "tensor"),
        P("tensor"),
        P("tensor", ("group", "dp")),
    )
    return jax.shard_map(shards, mesh=mesh, in_specs=in_specs, out_specs=out_specs, check_vma=False)
```

profile of v0, /device:TPU:2, one launch (start us, length us, event | category | flops | bytes accessed | tf_op | source)
XLA Modules:
  0.0 262.3 jit_solution(6069590258174314049)
XLA Ops:
  0.6 1.2 broadcast_in_dim.20
  1.8 64.8 %all_to_all.35 = bf16[32,64,480]{2,1,0:T(8,128)(2,1)S(1)} all-to-all(bf16[32,64,480]{2,1,0:T(8,128)(2,1)S(1)} %broadcast_in_dim.20), channel_id=1, replica_groups=mesh['group'=2,'dp'=8,'tensor'=32] {'tensor'}, dimensions={0} | all-to-all | bytes 3932160 | tf_op jit(solution)/shard_map/all_to_all | solution.py:19
  66.6 1.7 convolution_convert_fusion.1
  68.3 7.9 %all-to-all-start.1 = ((bf16[16,128,256]{2,1,0:T(8,128)(2,1)}), bf16[16,128,256]{2,1,0:T(8,128)(2,1)S(1)}, u32[]{:S(2)}, u32[]{:S(2)}) async-start(bf16[16,128,256]{2,1,0:T(8,128)(2,1)} %bitcast.1), calls=%async_computation.1 | async-start | bytes 2097152 | tf_op jit(solution)/shard_map/all_to_all | solution.py:36
  76.3 25.2 %all-to-all-done.1 = bf16[16,128,256]{2,1,0:T(8,128)(2,1)S(1)} async-done(((bf16[16,128,256]{2,1,0:T(8,128)(2,1)}), bf16[16,128,256]{2,1,0:T(8,128)(2,1)S(1)}, u32[]{:S(2)}, u32[]{:S(2)}) %all-to-all-start.1) | async-done | bytes 1048608 | tf_op jit(solution)/shard_map/all_to_all | solution.py:36
  102.2 35.2 %all_to_all.36 = f32[32,128,64]{1,2,0:T(8,128)S(1)} all-to-all(f32[32,128,64]{1,2,0:T(8,128)S(1)} %bitcast.104), channel_id=1, replica_groups=mesh['group'=2,'dp'=8,'tensor'=32] {'tensor'}, dimensions={0} | all-to-all | bytes 2097152 | tf_op jit(solution)/shard_map/all_to_all | solution.py:42
  137.5 0.9 broadcast_in_dim.21
  138.5 6.4 %all-to-all-start.3 = ((bf16[32,128,64]{1,2,0:T(8,128)(2,1)}), bf16[32,128,64]{1,2,0:T(8,128)(2,1)S(1)}, u32[]{:S(2)}, u32[]{:S(2)}) async-start(bf16[32,128,64]{1,2,0:T(8,128)(2,1)} %broadcast_in_dim.21), calls=%async_computation.3 | async-start | bytes 1048576 | tf_op jit(solution)/shard_map/all_to_all | solution.py:19
  145.3 15.9 %all-to-all-done.3 = bf16[32,128,64]{1,2,0:T(8,128)(2,1)S(1)} async-done(((bf16[32,128,64]{1,2,0:T(8,128)(2,1)}), bf16[32,128,64]{1,2,0:T(8,128)(2,1)S(1)}, u32[]{:S(2)}, u32[]{:S(2)}) %all-to-all-start.3) | async-done | bytes 524320 | tf_op jit(solution)/shard_map/all_to_all | solution.py:19
  162.4 2.2 collective-permute-start
  164.6 1.1 collective-permute-done
  165.7 3.7 %collective-permute-start.1 = (f32[128,256]{0,1:T(8,128)S(1)}, f32[128,256]{0,1:T(8,128)S(1)}, u32[]{:S(2)}, u32[]{:S(2)}) collective-permute-start(f32[128,256]{0,1:T(8,128)S(1)} %fusion.47), channel_id=1, source_target_pairs={{0,2},{1,3},{2,0},{3,1},{4,6},{5,7},{6,4},{7,5},{8,10},{9,11},{10,... | collective-permute-start | bytes 393224 | tf_op jit(solution)/shard_map/ppermute | solution.py:47
  169.4 4.0 %collective-permute-done.1 = f32[128,256]{0,1:T(8,128)S(1)} collective-permute-done((f32[128,256]{0,1:T(8,128)S(1)}, f32[128,256]{0,1:T(8,128)S(1)}, u32[]{:S(2)}, u32[]{:S(2)}) %collective-permute-start.1) | collective-permute-done | bytes 131104 | tf_op jit(solution)/shard_map/ppermute | solution.py:47
  173.5 22.2 %all_to_all.37 = bf16[32,128,64]{1,2,0:T(8,128)(2,1)S(1)} all-to-all(bf16[32,128,64]{1,2,0:T(8,128)(2,1)S(1)} %broadcast_in_dim.24), channel_id=1, replica_groups=mesh['group'=2,'dp'=8,'tensor'=32] {'tensor'}, dimensions={0} | all-to-all | bytes 1048576 | tf_op jit(solution)/shard_map/all_to_all | solution.py:19
  196.2 1.1 broadcast_in_dim.25
  197.3 4.7 %all-to-all-start.5 = ((bf16[16,128,256]{2,1,0:T(8,128)(2,1)}), bf16[16,128,256]{2,1,0:T(8,128)(2,1)S(1)}, u32[]{:S(2)}, u32[]{:S(2)}) async-start(bf16[16,128,256]{2,1,0:T(8,128)(2,1)} %broadcast_in_dim.25), calls=%async_computation.5 | async-start | bytes 2097152 | tf_op jit(solution)/shard_map/all_to_all | solution.py:19
  202.5 1.3 copy.87
  203.8 26.1 %all-to-all-done.5 = bf16[16,128,256]{2,1,0:T(8,128)(2,1)S(1)} async-done(((bf16[16,128,256]{2,1,0:T(8,128)(2,1)}), bf16[16,128,256]{2,1,0:T(8,128)(2,1)S(1)}, u32[]{:S(2)}, u32[]{:S(2)}) %all-to-all-start.5) | async-done | bytes 1048608 | tf_op jit(solution)/shard_map/all_to_all | solution.py:19
  229.8 4.3 %all-to-all-start.6 = ((bf16[16,256,128]{2,1,0:T(8,128)(2,1)}), bf16[16,256,128]{2,1,0:T(8,128)(2,1)S(1)}, u32[]{:S(2)}, u32[]{:S(2)}) async-start(bf16[16,256,128]{2,1,0:T(8,128)(2,1)} %bitcast.100), calls=%async_computation.6 | async-start | bytes 2097152 | tf_op jit(solution)/shard_map/all_to_all | solution.py:36
  234.2 1.9 convolution_convert_fusion.4
  236.0 1.7 copy.71
  237.7 1.3 convolution_convert_fusion.3
  240.6 3.2 %fusion.10 = bf16[480,256]{1,0:T(8,128)(2,1)} fusion(bf16[2048,256]{1,0:T(8,128)(2,1)S(1)} %bitcast.103, bf16[2048,480]{1,0:T(8,128)(2,1)} %bitcast.106), kind=kOutput, calls=%fused_computation.17 | convolution fusion | flops 503439360 | bytes 3260416 | tf_op jit(solution)/shard_map/dot_general | solution.py:118
  243.8 17.7 %all-to-all-done.6 = bf16[16,256,128]{2,1,0:T(8,128)(2,1)S(1)} async-done(((bf16[16,256,128]{2,1,0:T(8,128)(2,1)}), bf16[16,256,128]{2,1,0:T(8,128)(2,1)S(1)}, u32[]{:S(2)}, u32[]{:S(2)}) %all-to-all-start.6) | async-done | bytes 1048608 | tf_op jit(solution)/shard_map/all_to_all | solution.py:36
  (47 shorter events, 5.8 us)
Async XLA Ops:
  0.6 101.0 %copy-start = (bf16[256,2048]{1,0:T(8,128)(2,1)S(1)}, bf16[256,2048]{1,0:T(8,128)(2,1)}, u32[]{:S(2)}) copy-start(bf16[256,2048]{1,0:T(8,128)(2,1)} %param.11) | copy-start | bytes 3145732
  1.8 64.8 %copy-start.10 = (bf16[480,256]{1,0:T(8,128)(2,1)S(1)}, bf16[480,256]{1,0:T(8,128)(2,1)}, u32[]{:S(2)}) copy-start(bf16[480,256]{1,0:T(8,128)(2,1)} %param.9) | copy-start | bytes 737284
  66.6 1.7 copy-start.1
  68.3 7.9 %copy-start.11 = (bf16[256]{0:T(256)(128)(2,1)S(1)}, bf16[256]{0:T(256)(128)(2,1)}, u32[]{:S(2)}) copy-start(bf16[256]{0:T(256)(128)(2,1)} %param.10) | copy-start | bytes 1540
  68.3 33.2 %all-to-all-start.1 = ((bf16[16,128,256]{2,1,0:T(8,128)(2,1)}), bf16[16,128,256]{2,1,0:T(8,128)(2,1)S(1)}, u32[]{:S(2)}, u32[]{:S(2)}) async-start(bf16[16,128,256]{2,1,0:T(8,128)(2,1)} %bitcast.1), calls=%async_computation.1 | async-start | bytes 2097152 | tf_op jit(solution)/shard_map/all_to_all | solution.py:36
  102.2 42.7 %copy-start.3 = (bf16[256,256]{1,0:T(8,128)(2,1)S(1)}, bf16[256,256]{1,0:T(8,128)(2,1)}, u32[]{:S(2)}) copy-start(bf16[256,256]{1,0:T(8,128)(2,1)} %param.12) | copy-start | bytes 393220
  102.2 42.8 %copy-start.4 = (bf16[256,256]{1,0:T(8,128)(2,1)S(1)}, bf16[256,256]{1,0:T(8,128)(2,1)}, u32[]{:S(2)}) copy-start(bf16[256,256]{1,0:T(8,128)(2,1)} %param.13) | copy-start | bytes 393220
  137.5 7.7 %copy-start.8 = (s32[1,256]{1,0:T(1,128)S(1)}, s32[1,256]{1,0:T(1,128)}, u32[]{:S(2)}) copy-start(s32[1,256]{1,0:T(1,128)} %param.15) | copy-start | bytes 3076
  137.5 7.7 %copy-start.9 = (s32[1,128]{1,0:T(1,128)S(1)}, s32[1,128]{1,0:T(1,128)}, u32[]{:S(2)}) copy-start(s32[1,128]{1,0:T(1,128)} %param.14) | copy-start | bytes 1540
  138.5 22.7 %all-to-all-start.3 = ((bf16[32,128,64]{1,2,0:T(8,128)(2,1)}), bf16[32,128,64]{1,2,0:T(8,128)(2,1)S(1)}, u32[]{:S(2)}, u32[]{:S(2)}) async-start(bf16[32,128,64]{1,2,0:T(8,128)(2,1)} %broadcast_in_dim.21), calls=%async_computation.3 | async-start | bytes 1048576 | tf_op jit(solution)/shard_map/all_to_all | solution.py:19
  145.0 19.6 %copy-start.5 = (bf16[256,256]{0,1:T(8,128)(2,1)}, bf16[256,256]{0,1:T(8,128)(2,1)S(1)}, u32[]{:S(2)}) copy-start(bf16[256,256]{0,1:T(8,128)(2,1)S(1)} %copy.83) | copy-start | bytes 393220
  145.2 17.1 %copy-start.7 = (pred[256,128]{0,1:T(8,128)(4,1)}, pred[256,128]{0,1:T(8,128)(4,1)S(1)}, u32[]{:S(2)}) copy-start(pred[256,128]{0,1:T(8,128)(4,1)S(1)} %broadcast_compare_fusion) | copy-start | bytes 98308
  161.2 4.5 %copy-start.2 = (bf16[32,128,64]{1,2,0:T(8,128)(2,1)}, bf16[32,128,64]{1,2,0:T(8,128)(2,1)S(1)}, u32[]{:S(2)}) copy-start(bf16[32,128,64]{1,2,0:T(8,128)(2,1)S(1)} %all-to-all-done.3) | copy-start | bytes 1572868
  161.7 34.0 %copy-start.12 = (f32[2,256,128]{1,2,0:T(8,128)}, f32[2,256,128]{1,2,0:T(8,128)S(1)}, u32[]{:S(2)}) copy-start(f32[2,256,128]{1,2,0:T(8,128)S(1)} %get-tuple-element.26) | copy-start | bytes 786436
  162.4 3.2 %collective-permute-start = (f32[128,256]{0,1:T(8,128)S(1)}, f32[128,256]{0,1:T(8,128)S(1)}, u32[]{:S(2)}, u32[]{:S(2)}) collective-permute-start(f32[128,256]{0,1:T(8,128)S(1)} %pad_maximum_fusion), channel_id=1, source_target_pairs={{0,1},{1,0},{2,3},{3,2},{4,5},{5,4},{6,7},{7,6},{8,9},{9,8},{10,11... | collective-permute-start | bytes 393224 | tf_op jit(solution)/shard_map/ppermute | solution.py:47
  165.7 7.7 %collective-permute-start.1 = (f32[128,256]{0,1:T(8,128)S(1)}, f32[128,256]{0,1:T(8,128)S(1)}, u32[]{:S(2)}, u32[]{:S(2)}) collective-permute-start(f32[128,256]{0,1:T(8,128)S(1)} %fusion.47), channel_id=1, source_target_pairs={{0,2},{1,3},{2,0},{3,1},{4,6},{5,7},{6,4},{7,5},{8,10},{9,11},{10,... | collective-permute-start | bytes 393224 | tf_op jit(solution)/shard_map/ppermute | solution.py:47
  197.3 32.5 %all-to-all-start.5 = ((bf16[16,128,256]{2,1,0:T(8,128)(2,1)}), bf16[16,128,256]{2,1,0:T(8,128)(2,1)S(1)}, u32[]{:S(2)}, u32[]{:S(2)}) async-start(bf16[16,128,256]{2,1,0:T(8,128)(2,1)} %broadcast_in_dim.25), calls=%async_computation.5 | async-start | bytes 2097152 | tf_op jit(solution)/shard_map/all_to_all | solution.py:19
  202.5 31.6 %copy-start.6 = (bf16[256,256]{0,1:T(8,128)(2,1)S(1)}, bf16[256,256]{0,1:T(8,128)(2,1)}, u32[]{:S(2)}) copy-start(bf16[256,256]{0,1:T(8,128)(2,1)} %copy-done.5) | copy-start | bytes 393220
  229.8 31.6 %all-to-all-start.6 = ((bf16[16,256,128]{2,1,0:T(8,128)(2,1)}), bf16[16,256,128]{2,1,0:T(8,128)(2,1)S(1)}, u32[]{:S(2)}, u32[]{:S(2)}) async-start(bf16[16,256,128]{2,1,0:T(8,128)(2,1)} %bitcast.100), calls=%async_computation.6 | async-start | bytes 2097152 | tf_op jit(solution)/shard_map/all_to_all | solution.py:36
where the time goes:
time: 263 us; the launch traced here: 262 us
  blocking collectives  122 us (46%)
  waiting for transfers between devices  89.9 us (34%)
  starting transfers between devices  29.3 us (11%)
  matrix products  10.7 us (4%)
  local copies, waits for them, and re-layouts  7.25 us (3%)
    all_to_all x2, blocking collectives, from_everyone(): lax.all_to_all(jnp.broadcast_to(shard[None], (devices, *shard.shape)), ax...  86.9 us
    all_to_all x2, waiting for transfers between devices, sent_and_summed(): lax.all_to_all(split_up(shard, dim, devices), axis, 0, 0, tiled=True)  42.9 us
    all_to_all x2, waiting for transfers between devices, from_everyone(): lax.all_to_all(jnp.broadcast_to(shard[None], (devices, *shard.shape)), ax...  42 us
    all_to_all x1, blocking collectives, sum_at_owner(): lax.all_to_all(split_up(shard, dim, devices), axis, 0, 0, tiled=True)  35.2 us
    all_to_all x2, starting transfers between devices, sent_and_summed(): lax.all_to_all(split_up(shard, dim, devices), axis, 0, 0, tiled=True)  12.2 us
    all_to_all x2, starting transfers between devices, from_everyone(): lax.all_to_all(jnp.broadcast_to(shard[None], (devices, *shard.shape)), ax...  11.1 us
    ppermute x2, starting transfers between devices, from_partner(): lax.ppermute(shard, axis, [(i, i ^ 1 << distance) for i in range(lax.axis...  5.9 us
  transfers between devices with their start and end apart: 6, of which 6 were waited for; matrix products, arithmetic and copies ran while one was open for 4% of the time, Pallas kernels for 0%

commit v1 on v0

v1 whole, which is shorter than its diff:
```python
import jax
import jax.numpy as jnp
from jax import lax
from jax.experimental import pallas as pl
from jax.experimental.pallas import tpu as pltpu
from jax.sharding import PartitionSpec as P

MESH = pl.DeviceIdType.MESH
BF = jnp.bfloat16
F32 = jnp.float32
HD = 128
KVH = 8
SCALE = HD ** (-0.5)


def dot(a, b, ca=1, cb=0):
    return lax.dot_general(a, b, (((ca,), (cb,)), ((), ())), preferred_element_type=F32)


class Names:
    def __init__(self):
        self.slots = {}

    def __getitem__(self, name):
        return self.slots.setdefault(name, len(self.slots))


SLOTS = 160


def kernel(
    feat_ref, w_ref, bias_ref, kvw_ref, q_ref, g_ref, img_ref, txt_ref,
    att_ref, dq_ref, dw_ref, db_ref, dkw_ref,
    F, FT, W, own, KT, sh, sw, rh, rw, zb, proj, projT, sh2, sw2, rh2, rw2, held, zs, zr_,
    kvp, kvr, sx, rx, sz, rz, kvg, dks, dkr, D, G, ssem, rsem,
):
    zl = lax.axis_index("group")
    y = lax.axis_index("dp")
    t = lax.axis_index("tensor")
    zh = t // 8
    x = (t // 2) % 4
    c = t % 2

    def T(zr=0, xr=0, cr=0):
        return ((zh + zr) % 4) * 8 + ((x + xr) % 4) * 2 + (c + cr) % 2

    xf = x + 1 - 2 * (x % 2)

    def TF(cr):
        return zh * 8 + xf * 2 + (c + cr) % 2

    zdev = {r: {"tensor": T(zr=r)} for r in (1, 2, 3)}
    xdev = {r: {"tensor": T(xr=r)} for r in (1, 2, 3)}
    core = {"tensor": T(cr=1)}
    ydev = {1: {"dp": (y + 1) % 8}, -1: {"dp": (y + 7) % 8}}
    twin = {"group": 1 - zl}
    flips = ({"tensor": T(cr=1)}, {"tensor": TF(0)}, {"tensor": TF(1)})

    names = Names()
    sends = []

    def send(src, dst, name, dev):
        k = names[name]
        copy = pltpu.make_async_remote_copy(
            src_ref=src, dst_ref=dst, send_sem=ssem.at[k], recv_sem=rsem.at[k],
            device_id=dev, device_id_type=MESH,
        )
        copy.start()
        sends.append(copy)

    def arrive(ref, name):
        k = names[name]
        pltpu.make_async_remote_copy(
            src_ref=ref, dst_ref=ref, send_sem=ssem.at[k], recv_sem=rsem.at[k],
            device_id=core, device_id_type=MESH,
        ).wait_recv()

    barrier = pltpu.get_barrier_semaphore()
    peers = [*zdev.values(), *xdev.values(), *ydev.values(), twin, core, flips[2]]
    for dev in peers:
        pl.semaphore_signal(barrier, inc=1, device_id=dev, device_id_type=MESH)

    own[...] = jnp.zeros_like(own)
    own[:, 0:480] = feat_ref[...]
    F[t] = own[...]
    W[480:512, :] = jnp.zeros((32, 256), BF)
    W[0:480, :] = w_ref[...]

    pl.semaphore_wait(barrier, len(peers))

    up, down = slice(0, 32), slice(32, 64)

    def spread(zr):
        ref = F.at[T(zr=zr)]
        send(ref, ref, f"x+{zr}", xdev[1])
        send(ref, ref, f"x-{zr}", xdev[3])

    def share(zr, xr):
        ref = F.at[T(zr, xr)]
        send(ref, ref, f"c{zr}{xr}", core)

    send(F.at[t], F.at[t], "z+", zdev[1])
    send(F.at[t], F.at[t], "z-", zdev[3])
    spread(0)
    share(0, 0)

    def bend(zr):
        for step, rows, to in ((3, up, 1), (1, down, 3)):
            ref = F.at[T(zr, step)]
            arrive(ref, f"x+{zr}" if step == 3 else f"x-{zr}")
            half = F.at[T(zr, step), rows]
            send(half, half, f"h{step}{zr}", xdev[to])
            share(zr, step)

    def last(zr):
        arrive(F.at[T(zr, 2), up], f"h3{zr}")
        arrive(F.at[T(zr, 2), down], f"h1{zr}")
        share(zr, 2)

    for h in range(KVH):
        for half in range(2):
            cols = pl.ds(half * 1024 + h * HD, HD)
            KT[h, pl.ds(half * HD, HD), :] = kvw_ref[:, cols].T

    arrive(F.at[T(3)], "z+")
    half = F.at[T(3), up]
    send(half, half, "zh3", zdev[1])
    spread(3)
    share(3, 0)
    arrive(F.at[T(1)], "z-")
    half = F.at[T(1), down]
    send(half, half, "zh1", zdev[3])
    spread(1)
    share(1, 0)
    bend(0)
    arrive(F.at[T(2), up], "zh3")
    arrive(F.at[T(2), down], "zh1")
    spread(2)
    share(2, 0)
    bend(3)
    bend(1)
    last(0)
    bend(2)
    last(3)
    last(1)
    last(2)
    for zr in range(4):
        for xr in range(4):
            arrive(F.at[T(zr, xr, 1)], f"c{zr}{xr}")

    def reduce_y(tag, tile, s_half, s_whole, r_half, r_whole, between=None):
        lanes = (slice(0, 128), slice(128, 256))
        for j in range(2):
            far = tile(j, (y + 4) % 8)
            for d, way in enumerate((1, -1)):
                s_half[d, j] = far[:, lanes[d]].astype(BF)
                send(s_half.at[d, j], r_half.at[d, j], f"{tag}{d}{j}0", ydev[way])
        for k in (1, 2, 3):
            if between is not None:
                between(k)
            for j in range(2):
                for d, way in enumerate((1, -1)):
                    part = tile(j, (y + way * (4 - k) + 8) % 8)
                    if k == 1:
                        arrive(r_half.at[d, j], f"{tag}{d}{j}0")
                        halves = [part[:, lanes[0]], part[:, lanes[1]]]
                        halves[d] = halves[d] + r_half[d, j].astype(F32)
                        for l in range(2):
                            s_whole[d, j, 0, :, lanes[l]] = halves[l].astype(BF)
                    else:
                        arrive(r_whole.at[d, j, k - 2], f"{tag}{d}{j}{k - 1}")
                        s_whole[d, j, k - 1] = (part + r_whole[d, j, k - 2].astype(F32)).astype(BF)
                    send(s_whole.at[d, j, k - 1], r_whole.at[d, j, k - 1], f"{tag}{d}{j}{k}", ydev[way])

    def settle_y(tag, j, tile, r_whole):
        total = tile(j, y)
        for d in range(2):
            arrive(r_whole.at[d, j, 2], f"{tag}{d}{j}3")
            total = total + r_whole[d, j, 2].astype(F32)
        return total

    def partial(j, row):
        shard = ((1 - zl if j == 0 else zl) * 8 + row) * 2
        rows = F[pl.ds(shard, 2)].reshape(128, 512)
        return dot(rows, W[...])

    reduce_y("p", partial, sh, sw, rh, rw)
    zb[0] = settle_y("p", 0, partial, rw).astype(BF)
    send(zb.at[0], zb.at[1], "pz", twin)
    total = settle_y("p", 1, partial, rw) + bias_ref[...].astype(F32)
    arrive(zb.at[1], "pz")
    projected = (total + zb[1].astype(F32)).astype(BF)
    proj[...] = projected

    for h in range(KVH):
        for half in range(2):
            cols = pl.ds(half * 1024 + h * HD, HD)
            block = dot(projected, kvw_ref[:, cols]).astype(BF)
            for m in range(4):
                kvp[m % 2, (h % 2) * 2 + m // 2, h // 2, :, pl.ds(half * HD, HD)] = block[32 * m : 32 * m + 32]
    send(kvp.at[1 - c], kvr, "kc", core)
    projT[...] = projected.T
    arrive(kvr, "kc")
    sx[...] = (kvp[c].astype(F32) + kvr[...].astype(F32)).astype(BF)
    for r in (2, 1, 3):
        send(sx.at[(x + r) % 4], rx.at[r - 1], f"kx{r}", xdev[r])

    def turn(lo, hi):
        def body(s, carry):
            rows = F[pl.ds(s * 2, 2)].reshape(128, 512)
            FT[:, pl.ds(pl.multiple_of(s * 128, 128), 128)] = rows.T
            return carry

        lax.fori_loop(lo, hi, body, 0)

    turn(0, 4)
    acc = sx[x].astype(F32)
    for r in (1, 3, 2):
        arrive(rx.at[r - 1], f"kx{r}")
        acc = acc + rx[r - 1].astype(F32)
    sz[...] = acc.astype(BF)
    for r in (2, 1, 3):
        send(sz.at[(zh + r) % 4], rz.at[r - 1], f"kz{r}", zdev[r])
    turn(4, 8)
    acc = sz[zh].astype(F32)
    for r in (1, 3, 2):
        arrive(rz.at[r - 1], f"kz{r}")
        acc = acc + rz[r - 1].astype(F32)
    m = (x % 2) * 2 + c
    kvg[m] = acc.astype(BF)
    for f, dev in enumerate(flips):
        send(kvg.at[m], kvg.at[m], f"kg{f}", dev)
    mates = ((x % 2) * 2 + 1 - c, (1 - x % 2) * 2 + c, (1 - x % 2) * 2 + 1 - c)
    for f in range(3):
        arrive(kvg.at[mates[f]], f"kg{f}")
    both = kvg[...].reshape(HD, 2 * HD)
    keys, values = both[:, :HD], both[:, HD:]

    allowed = txt_ref[...] == img_ref[...]
    dk = jnp.zeros((HD, HD), F32)
    dv = jnp.zeros((HD, HD), F32)
    for head in range(2):
        cols = slice(head * HD, head * HD + HD)
        q, g = q_ref[:, cols], g_ref[:, cols]
        scores = dot(q, keys, 1, 1) * SCALE
        scores = jnp.where(allowed, scores, F32(-1e30))
        expo = jnp.exp(scores - jnp.max(scores, axis=-1, keepdims=True))
        probs = expo / jnp.sum(expo, axis=-1, keepdims=True)
        probs_b = probs.astype(BF)
        att_ref[:, cols] = dot(probs_b, values).astype(BF)
        dprobs = dot(g, values, 1, 1)
        delta = jnp.sum(probs * dprobs, axis=-1, keepdims=True)
        dscores = (probs * (dprobs - delta) * SCALE).astype(BF)
        dq_ref[:, cols] = dot(dscores, keys).astype(BF)
        dk = dk + dot(dscores, q, 0, 0)
        dv = dv + dot(probs_b, g, 0, 0)

    stacked = jnp.concatenate([dk, dv], axis=1)
    dks[...] = stacked.reshape(4, 32, 2 * HD).astype(BF)
    for f, dev in enumerate(flips):
        send(dks.at[mates[f]], dkr.at[f], f"dk{f}", dev)
    mine = dks[m].astype(F32)
    for f in range(3):
        arrive(dkr.at[f], f"dk{f}")
        mine = mine + dkr[f].astype(F32)
    D[t] = mine.astype(BF)
    own_d = D.at[t]
    for r in (2, 1, 3):
        send(own_d, own_d, f"dz{r}", zdev[r])
    for r in (2, 1, 3):
        send(own_d, own_d, f"dx0{r}", xdev[r])
    send(own_d, own_d, "dc00", core)
    turn(8, 12)
    for r in (1, 3, 2):
        ref = D.at[T(4 - r)]
        arrive(ref, f"dz{r}")
        for s in (2, 1, 3):
            send(ref, ref, f"dx{4 - r}{s}", xdev[s])
        send(ref, ref, f"dc{4 - r}0", core)
    for zr in (0, 3, 1, 2):
        for s in (1, 3, 2):
            ref = D.at[T(zr, 4 - s)]
            arrive(ref, f"dx{zr}{s}")
            send(ref, ref, f"dc{zr}{4 - s}", core)
    for zr in range(4):
        for xr in range(4):
            arrive(D.at[T(zr, xr, 1)], f"dc{zr}{xr}")

    grad = jnp.zeros((128, 256), F32)
    for h in range(KVH):
        grad = grad + dot(D[4 * h : 4 * h + 4].reshape(128, 256), KT[h])

    def G_at(zr, yr):
        side = zl if zr == 0 else 1 - zl
        return G.at[side * 8 + (y + yr + 8) % 8]

    G[zl * 8 + y] = grad.astype(BF)
    piece = G_at(0, 0)
    send(piece, piece, "g+1", ydev[1])
    send(piece, piece, "g-1", ydev[-1])
    send(piece, piece, "gz0", twin)

    def weight_part(j, row):
        rows = D[pl.ds(row * 4, 4)].reshape(128, 256)
        return dot(projT[j * 128 : j * 128 + 128, :], rows)

    def pass_on(k):
        for way, sign, rows in ((1, "+", slice(0, 64)), (-1, "-", slice(64, 128))):
            piece = G_at(0, -way * k)
            arrive(piece, f"g{sign}{k}")
            if k < 3:
                send(piece, piece, f"g{sign}{k + 1}", ydev[way])
            else:
                index = zl * 8 + (y - way * k + 8) % 8
                send(G.at[index, rows], G.at[index, rows], f"g{sign}4", ydev[way])
            send(piece, piece, f"gz{sign}{k}", twin)

    reduce_y("w", weight_part, sh2, sw2, rh2, rw2, pass_on)
    turn(12, 16)
    opposite = zl * 8 + (y + 4) % 8
    arrive(G.at[opposite, slice(0, 64)], "g+4")
    arrive(G.at[opposite, slice(64, 128)], "g-4")
    send(G.at[opposite], G.at[opposite], "gz4", twin)
    mine_cols = pl.ds(pl.multiple_of(zl * 128, 128), 128)
    twin_cols = pl.ds(pl.multiple_of((1 - zl) * 128, 128), 128)
    for j in range(2):
        held[j] = settle_y("w", j, weight_part, rw2)
        zs[j] = held[j, :, twin_cols].astype(BF)
        send(zs.at[j], zr_.at[j], f"wz{j}", twin)

    def weight_grad(side):
        rows = G[pl.ds(side * 8, 8)].reshape(1024, 256)
        features = FT[:, pl.ds(pl.multiple_of(side * 1024, 1024), 1024)]
        return dot(features, rows), jnp.sum(rows.astype(F32), axis=0, keepdims=True)

    grad_w, grad_b = weight_grad(zl)
    for j in range(2):
        arrive(zr_.at[j], f"wz{j}")
        dkw_ref[j * 128 : j * 128 + 128, :] = (held[j, :, mine_cols] + zr_[j].astype(F32)).astype(BF)
    arrive(G_at(1, 0), "gz0")
    for k in (1, 2, 3):
        arrive(G_at(1, -k), f"gz+{k}")
        arrive(G_at(1, k), f"gz-{k}")
    arrive(G_at(1, 4), "gz4")
    more_w, more_b = weight_grad(1 - zl)
    dw_ref[...] = (grad_w + more_w)[0:480].astype(BF)
    db_ref[...] = grad_b + more_b
    for copy in sends:
        copy.wait_send()
    assert len(names.slots) <= SLOTS, len(names.slots)


def shards(
    image_feats, proj_weight, proj_bias, kv_weight, queries, out_grad, image_sample, text_sample
):
    vm = pltpu.VMEM
    out = pl.pallas_call(
        kernel,
        out_shape=(
            jax.ShapeDtypeStruct((256, 256), BF),
            jax.ShapeDtypeStruct((256, 256), BF),
            jax.ShapeDtypeStruct((480, 256), BF),
            jax.ShapeDtypeStruct((1, 256), F32),
            jax.ShapeDtypeStruct((256, 128), BF),
        ),
        in_specs=[pl.BlockSpec(memory_space=vm)] * 8,
        out_specs=[pl.BlockSpec(memory_space=vm)] * 5,
        scratch_shapes=[
            vm((32, 64, 512), BF),
            vm((512, 2048), BF),
            vm((512, 256), BF),
            vm((64, 512), BF),
            vm((KVH, 256, 256), BF),
            vm((2, 2, 128, 128), BF),
            vm((2, 2, 3, 128, 256), BF),
            vm((2, 2, 128, 128), BF),
            vm((2, 2, 3, 128, 256), BF),
            vm((2, 128, 256), BF),
            vm((128, 256), BF),
            vm((256, 128), BF),
            vm((2, 2, 128, 128), BF),
            vm((2, 2, 3, 128, 256), BF),
            vm((2, 2, 128, 128), BF),
            vm((2, 2, 3, 128, 256), BF),
            vm((2, 128, 256), F32),
            vm((2, 128, 128), BF),
            vm((2, 128, 128), BF),
            vm((2, 4, 4, 32, 256), BF),
            vm((4, 4, 32, 256), BF),
            vm((4, 4, 32, 256), BF),
            vm((3, 4, 32, 256), BF),
            vm((4, 32, 256), BF),
            vm((3, 32, 256), BF),
            vm((4, 32, 256), BF),
            vm((4, 32, 256), BF),
            vm((3, 32, 256), BF),
            vm((32, 32, 256), BF),
            vm((16, 128, 256), BF),
            pltpu.SemaphoreType.DMA((SLOTS,)),
            pltpu.SemaphoreType.DMA((SLOTS,)),
        ],
        compiler_params=pltpu.CompilerParams(
            collective_id=0, has_side_effects=True, vmem_limit_bytes=48 * 2**20
        ),
        name="layer",
    )(
        image_feats, proj_weight, proj_bias.reshape(1, 256), kv_weight, queries, out_grad,
        image_sample, text_sample.reshape(256, 1),
    )
    attended, d_queries, d_proj, d_bias, d_kv = out
    return attended, d_queries, d_proj, d_bias.reshape(256), d_kv


def solution(mesh):
    in_specs = (
        P("tensor", ("group", "dp")),
        P(("group", "dp"), "tensor"),
        P("tensor"),
        P("tensor", None),
        P(("group", "dp"), "tensor"),
        P(("group", "dp"), "tensor"),
        P(("group", "dp"), None),
        P(("group", "dp"), None),
    )
    out_specs = (
        P(("group", "dp"), "tensor"),
        P(("group", "dp"), "tensor"),
        P(("group", "dp"), "tensor"),
        P("tensor"),
        P("tensor", ("group", "dp")),
    )
    return jax.shard_map(shards, mesh=mesh, in_specs=in_specs, out_specs=out_specs, check_vma=False)
```

time: 263 us -> 110 us (0.42)
  the two profiles are of different devices: /device:TPU:2 before, /device:TPU:64 now
where the time goes in v1:
time: 110 us
  Pallas kernels  100 us (91%)
  local copies, waits for them, and re-layouts  8.62 us (8%)
    pallas_call x1, Pallas kernels, shards(): pl.pallas_call(kernel, out_shape=(jax.ShapeDtypeStruct((256, 256), BF), j...  100 us
    unnamed x17, local copies, waits for them, and re-layouts  7.11 us

profile of v1, /device:TPU:64, one launch (start us, length us, event | category | flops | bytes accessed | tf_op | source)
XLA Modules:
  0.0 109.7 jit_solution(10813718671913847729)
XLA Ops:
  0.6 0.0 copy-start.2
  0.6 0.7 reshape.19.bias_ref
  1.3 0.0 copy-start.5
  1.3 0.8 copy.13.txt_ref
  2.2 0.0 copy-done.2
  2.2 0.0 copy-done.5
  2.2 0.0 copy-start
  2.2 1.2 %copy-done = bf16[256,2048]{1,0:T(8,128)(2,1)S(1)} copy-done((bf16[256,2048]{1,0:T(8,128)(2,1)S(1)}, bf16[256,2048]{1,0:T(8,128)(2,1)}, u32[]{:S(2)}) %copy-start) | copy-done | bytes 1048600
  3.4 0.0 copy-start.1
  3.4 0.9 copy-done.1
  4.4 0.0 copy-start.3
  4.4 0.9 copy-done.3
  5.3 0.0 copy-start.4
  5.3 0.8 copy-done.4
  6.1 100.4 %layer.1 = (bf16[256,256]{1,0:T(8,128)(2,1)S(1)}, bf16[256,256]{1,0:T(8,128)(2,1)S(1)}, bf16[480,256]{1,0:T(8,128)(2,1)S(1)}, f32[1,256]{1,0:T(1,128)S(1)}, bf16[256,128]{1,0:T(8,128)(2,1)S(1)}) custom-call(bf16[64,480]{1,0:T(8,128)(2,1)S(1)} %copy-done.4, bf16[480,256]{1,0:T(8,128)(2,1)S(1)} %copy-done.1, bf16[1,256]{1,0:T(2,128)(2,1)S(1)} %reshape.19.bias_ref, ...), custom_call_target="tpu_custom_call" | custom-call | tf_op jit(solution)/shard_map/layer/pallas_call | solution.py:357
  106.5 0.7 copy.19
  107.2 0.7 copy.20
  107.8 0.7 copy.21
  108.5 0.6 copy.22
  109.1 0.6 copy.23
Async XLA Ops:
  0.6 1.5 %copy-start.2 = (bf16[256,256]{1,0:T(8,128)(2,1)S(1)}, bf16[256,256]{1,0:T(8,128)(2,1)}, u32[]{:S(2)}) copy-start(bf16[256,256]{1,0:T(8,128)(2,1)} %q_ref.1) | copy-start | bytes 393220
  1.3 0.8 copy-start.5
  2.2 1.2 %copy-start = (bf16[256,2048]{1,0:T(8,128)(2,1)S(1)}, bf16[256,2048]{1,0:T(8,128)(2,1)}, u32[]{:S(2)}) copy-start(bf16[256,2048]{1,0:T(8,128)(2,1)} %kvw_ref.1) | copy-start | bytes 3145732
  3.4 0.9 copy-start.1
  4.4 0.9 copy-start.3
  5.3 0.8 copy-start.4

commit v2 on v1

--- a/solution.py
+++ b/solution.py
@@ -25,14 +25,18 @@
         return self.slots.setdefault(name, len(self.slots))
 
 
-SLOTS = 160
+SLOTS = 256
+VMEM_ALL = 67043328
+HALVES = (slice(0, 64), slice(64, 128))
 
 
 def kernel(
+    feat_in, w_in, bias_in, kvw_in, q_in, g_in, img_in, txt_in,
+    att_out, dq_out, dw_out, db_out, dkw_out,
+    F, FT, W, own, KT, sh, sw, rh, rw, zb, proj, projT, sh2, sw2, rh2, rw2, held, zs, zr_,
+    kvp, kvr, sx, rx, sz, rz, kvg, dks, dkr, D, G,
     feat_ref, w_ref, bias_ref, kvw_ref, q_ref, g_ref, img_ref, txt_ref,
-    att_ref, dq_ref, dw_ref, db_ref, dkw_ref,
-    F, FT, W, own, KT, sh, sw, rh, rw, zb, proj, projT, sh2, sw2, rh2, rw2, held, zs, zr_,
-    kvp, kvr, sx, rx, sz, rz, kvg, dks, dkr, D, G, ssem, rsem,
+    att_ref, dq_ref, dw_ref, db_ref, dkw_ref, ssem, rsem, lsem,
 ):
     zl = lax.axis_index("group")
     y = lax.axis_index("dp")
@@ -75,75 +79,115 @@
             device_id=core, device_id_type=MESH,
         ).wait_recv()
 
+    inputs = (feat_in, w_in, kvw_in, bias_in, q_in, g_in, img_in, txt_in)
+    places = (feat_ref, w_ref, kvw_ref, bias_ref, q_ref, g_ref, img_ref, txt_ref)
+    fetch = [pltpu.make_async_copy(a, b, lsem.at[i]) for i, (a, b) in enumerate(zip(inputs, places))]
+    for copy in fetch:
+        copy.start()
+
     barrier = pltpu.get_barrier_semaphore()
     peers = [*zdev.values(), *xdev.values(), *ydev.values(), twin, core, flips[2]]
     for dev in peers:
         pl.semaphore_signal(barrier, inc=1, device_id=dev, device_id_type=MESH)
 
     own[...] = jnp.zeros_like(own)
+    fetch[0].wait()
     own[:, 0:480] = feat_ref[...]
     F[t] = own[...]
-    W[480:512, :] = jnp.zeros((32, 256), BF)
-    W[0:480, :] = w_ref[...]
 
     pl.semaphore_wait(barrier, len(peers))
 
-    up, down = slice(0, 32), slice(32, 64)
-
-    def spread(zr):
-        ref = F.at[T(zr=zr)]
-        send(ref, ref, f"x+{zr}", xdev[1])
-        send(ref, ref, f"x-{zr}", xdev[3])
+    def piece(zr, xr, half):
+        return F.at[T(zr, xr), slice(32 * half, 32 * half + 32)]
+
+    def spread(zr, half):
+        ref = piece(zr, 0, half)
+        send(ref, ref, f"x+{zr}{half}", xdev[1])
+        send(ref, ref, f"x-{zr}{half}", xdev[3])
 
     def share(zr, xr):
         ref = F.at[T(zr, xr)]
         send(ref, ref, f"c{zr}{xr}", core)
 
-    send(F.at[t], F.at[t], "z+", zdev[1])
-    send(F.at[t], F.at[t], "z-", zdev[3])
-    spread(0)
+    send(piece(0, 0, 0), piece(0, 0, 0), "z+0", zdev[1])
+    send(piece(0, 0, 1), piece(0, 0, 1), "z-1", zdev[3])
+    send(piece(0, 0, 0), piece(0, 0, 0), "x+00", xdev[1])
+    send(piece(0, 0, 1), piece(0, 0, 1), "x-01", xdev[3])
+    send(piece(0, 0, 1), piece(0, 0, 1), "z+1", zdev[1])
+    send(piece(0, 0, 0), piece(0, 0, 0), "z-0", zdev[3])
+    send(piece(0, 0, 1), piece(0, 0, 1), "x+01", xdev[1])
+    send(piece(0, 0, 0), piece(0, 0, 0), "x-00", xdev[3])
     share(0, 0)
-
-    def bend(zr):
-        for step, rows, to in ((3, up, 1), (1, down, 3)):
-            ref = F.at[T(zr, step)]
-            arrive(ref, f"x+{zr}" if step == 3 else f"x-{zr}")
-            half = F.at[T(zr, step), rows]
-            send(half, half, f"h{step}{zr}", xdev[to])
-            share(zr, step)
+    for i in range(1, 8):
+        fetch[i].wait()
+    W[480:512, :] = jnp.zeros((32, 256), BF)
+    W[0:480, :] = w_ref[...]
+
+    def from_z(zr, half):
+        ref = piece(zr, 0, half)
+        if zr == 2:
+            arrive(ref, f"zf{half}")
+        else:
+            arrive(ref, f"z+{half}" if zr == 3 else f"z-{half}")
+            if (zr, half) == (3, 0):
+                send(ref, ref, "zf0", zdev[1])
+            if (zr, half) == (1, 1):
+                send(ref, ref, "zf1", zdev[3])
+        spread(zr, half)
+
+    def from_x(zr, xr, half):
+        ref = piece(zr, xr, half)
+        arrive(ref, f"x+{zr}{half}" if xr == 3 else f"x-{zr}{half}")
+        if (xr, half) == (3, 0):
+            send(ref, ref, f"xf0{zr}", xdev[1])
+        if (xr, half) == (1, 1):
+            send(ref, ref, f"xf1{zr}", xdev[3])
 
     def last(zr):
-        arrive(F.at[T(zr, 2), up], f"h3{zr}")
-        arrive(F.at[T(zr, 2), down], f"h1{zr}")
+        arrive(piece(zr, 2, 0), f"xf0{zr}")
+        arrive(piece(zr, 2, 1), f"xf1{zr}")
         share(zr, 2)
 
+    from_x(0, 3, 0)
+    from_x(0, 1, 1)
+    from_z(3, 0)
+    from_z(1, 1)
+    from_x(0, 3, 1)
+    from_x(0, 1, 0)
+    share(0, 3)
+    share(0, 1)
+    from_z(3, 1)
+    from_z(1, 0)
+    share(3, 0)
+    share(1, 0)
+    from_z(2, 0)
+    from_z(2, 1)
+    share(2, 0)
+    from_x(3, 3, 0)
+    from_x(1, 1, 1)
+    from_x(3, 1, 0)
+    from_x(1, 3, 1)
+    from_x(3, 1, 1)
+    from_x(1, 3, 0)
+    from_x(3, 3, 1)
+    from_x(1, 1, 0)
+    for zr in (3, 1):
+        share(zr, 3)
+        share(zr, 1)
+    last(0)
+    from_x(2, 3, 0)
+    from_x(2, 1, 1)
+    from_x(2, 3, 1)
+    from_x(2, 1, 0)
+    share(2, 3)
+    share(2, 1)
+    last(3)
+    last(1)
+    last(2)
     for h in range(KVH):
         for half in range(2):
             cols = pl.ds(half * 1024 + h * HD, HD)
             KT[h, pl.ds(half * HD, HD), :] = kvw_ref[:, cols].T
-
-    arrive(F.at[T(3)], "z+")
-    half = F.at[T(3), up]
-    send(half, half, "zh3", zdev[1])
-    spread(3)
-    share(3, 0)
-    arrive(F.at[T(1)], "z-")
-    half = F.at[T(1), down]
-    send(half, half, "zh1", zdev[3])
-    spread(1)
-    share(1, 0)
-    bend(0)
-    arrive(F.at[T(2), up], "zh3")
-    arrive(F.at[T(2), down], "zh1")
-    spread(2)
-    share(2, 0)
-    bend(3)
-    bend(1)
-    last(0)
-    bend(2)
-    last(3)
-    last(1)
-    last(2)
     for zr in range(4):
         for xr in range(4):
             arrive(F.at[T(zr, xr, 1)], f"c{zr}{xr}")
@@ -152,32 +196,37 @@
         lanes = (slice(0, 128), slice(128, 256))
         for j in range(2):
             far = tile(j, (y + 4) % 8)
-            for d, way in enumerate((1, -1)):
-                s_half[d, j] = far[:, lanes[d]].astype(BF)
-                send(s_half.at[d, j], r_half.at[d, j], f"{tag}{d}{j}0", ydev[way])
+            for n, rows in enumerate(HALVES):
+                for d, way in enumerate((1, -1)):
+                    s_half[d, j, rows, :] = far[rows, lanes[d]].astype(BF)
+                    send(s_half.at[d, j, rows], r_half.at[d, j, rows], f"{tag}{d}{j}{n}0", ydev[way])
         for k in (1, 2, 3):
             if between is not None:
                 between(k)
             for j in range(2):
-                for d, way in enumerate((1, -1)):
-                    part = tile(j, (y + way * (4 - k) + 8) % 8)
-                    if k == 1:
-                        arrive(r_half.at[d, j], f"{tag}{d}{j}0")
-                        halves = [part[:, lanes[0]], part[:, lanes[1]]]
-                        halves[d] = halves[d] + r_half[d, j].astype(F32)
-                        for l in range(2):
-                            s_whole[d, j, 0, :, lanes[l]] = halves[l].astype(BF)
-                    else:
-                        arrive(r_whole.at[d, j, k - 2], f"{tag}{d}{j}{k - 1}")
-                        s_whole[d, j, k - 1] = (part + r_whole[d, j, k - 2].astype(F32)).astype(BF)
-                    send(s_whole.at[d, j, k - 1], r_whole.at[d, j, k - 1], f"{tag}{d}{j}{k}", ydev[way])
-
-    def settle_y(tag, j, tile, r_whole):
-        total = tile(j, y)
+                parts = [tile(j, (y + way * (4 - k) + 8) % 8) for way in (1, -1)]
+                for n, rows in enumerate(HALVES):
+                    for d, way in enumerate((1, -1)):
+                        part = parts[d][rows]
+                        if k == 1:
+                            arrive(r_half.at[d, j, rows], f"{tag}{d}{j}{n}0")
+                            halves = [part[:, lanes[0]], part[:, lanes[1]]]
+                            halves[d] = halves[d] + r_half[d, j, rows, :].astype(F32)
+                            for l in range(2):
+                                s_whole[d, j, 0, rows, lanes[l]] = halves[l].astype(BF)
+                        else:
+                            got = r_whole.at[d, j, k - 2, rows]
+                            arrive(got, f"{tag}{d}{j}{n}{k - 1}")
+                            s_whole[d, j, k - 1, rows, :] = (part + got[...].astype(F32)).astype(BF)
+                        source = s_whole.at[d, j, k - 1, rows]
+                        send(source, r_whole.at[d, j, k - 1, rows], f"{tag}{d}{j}{n}{k}", ydev[way])
+
+    def settle_y(tag, j, tile, r_whole, n):
         for d in range(2):
-            arrive(r_whole.at[d, j, 2], f"{tag}{d}{j}3")
-            total = total + r_whole[d, j, 2].astype(F32)
-        return total
+            got = r_whole.at[d, j, 2, HALVES[n]]
+            arrive(got, f"{tag}{d}{j}{n}3")
+            tile = tile + got[...].astype(F32)
+        return tile
 
     def partial(j, row):
         shard = ((1 - zl if j == 0 else zl) * 8 + row) * 2
@@ -185,11 +234,16 @@
         return dot(rows, W[...])
 
     reduce_y("p", partial, sh, sw, rh, rw)
-    zb[0] = settle_y("p", 0, partial, rw).astype(BF)
-    send(zb.at[0], zb.at[1], "pz", twin)
-    total = settle_y("p", 1, partial, rw) + bias_ref[...].astype(F32)
-    arrive(zb.at[1], "pz")
-    projected = (total + zb[1].astype(F32)).astype(BF)
+    away = partial(0, y)
+    home = partial(1, y) + bias_ref[...].astype(F32).reshape(1, 256)
+    for n, rows in enumerate(HALVES):
+        zb[0, rows, :] = settle_y("p", 0, away[rows], rw, n).astype(BF)
+        send(zb.at[0, rows], zb.at[1, rows], f"pz{n}", twin)
+    settled = [settle_y("p", 1, home[rows], rw, n) for n, rows in enumerate(HALVES)]
+    for n, rows in enumerate(HALVES):
+        arrive(zb.at[1, rows], f"pz{n}")
+        settled[n] = settled[n] + zb[1, rows, :].astype(F32)
+    projected = jnp.concatenate(settled, axis=0).astype(BF)
     proj[...] = projected
 
     for h in range(KVH):
@@ -202,8 +256,9 @@
     projT[...] = projected.T
     arrive(kvr, "kc")
     sx[...] = (kvp[c].astype(F32) + kvr[...].astype(F32)).astype(BF)
-    for r in (2, 1, 3):
-        send(sx.at[(x + r) % 4], rx.at[r - 1], f"kx{r}", xdev[r])
+    for zr in (2, 1, 3, 0):
+        for r in (2, 1, 3):
+            send(sx.at[(x + r) % 4, (zh + zr) % 4], rx.at[r - 1, zr], f"kx{r}{zr}", xdev[r])
 
     def turn(lo, hi):
         def body(s, carry):
@@ -214,15 +269,15 @@
         lax.fori_loop(lo, hi, body, 0)
 
     turn(0, 4)
-    acc = sx[x].astype(F32)
-    for r in (1, 3, 2):
-        arrive(rx.at[r - 1], f"kx{r}")
-        acc = acc + rx[r - 1].astype(F32)
-    sz[...] = acc.astype(BF)
-    for r in (2, 1, 3):
-        send(sz.at[(zh + r) % 4], rz.at[r - 1], f"kz{r}", zdev[r])
+    for zr in (2, 1, 3, 0):
+        acc = sx[x, (zh + zr) % 4].astype(F32)
+        for r in (1, 3, 2):
+            arrive(rx.at[r - 1, zr], f"kx{r}{zr}")
+            acc = acc + rx[r - 1, zr].astype(F32)
+        if zr:
+            sz[zr] = acc.astype(BF)
+            send(sz.at[zr], rz.at[zr - 1], f"kz{zr}", zdev[zr])
     turn(4, 8)
-    acc = sz[zh].astype(F32)
     for r in (1, 3, 2):
         arrive(rz.at[r - 1], f"kz{r}")
         acc = acc + rz[r - 1].astype(F32)
@@ -230,13 +285,14 @@
     kvg[m] = acc.astype(BF)
     for f, dev in enumerate(flips):
         send(kvg.at[m], kvg.at[m], f"kg{f}", dev)
+    texts = jnp.broadcast_to(txt_ref[...].astype(F32), (HD, 256)).T
+    allowed = texts == img_ref[...].astype(F32)
     mates = ((x % 2) * 2 + 1 - c, (1 - x % 2) * 2 + c, (1 - x % 2) * 2 + 1 - c)
     for f in range(3):
         arrive(kvg.at[mates[f]], f"kg{f}")
     both = kvg[...].reshape(HD, 2 * HD)
     keys, values = both[:, :HD], both[:, HD:]
 
-    allowed = txt_ref[...] == img_ref[...]
     dk = jnp.zeros((HD, HD), F32)
     dv = jnp.zeros((HD, HD), F32)
     for head in range(2):
@@ -254,6 +310,16 @@
         dq_ref[:, cols] = dot(dscores, keys).astype(BF)
         dk = dk + dot(dscores, q, 0, 0)
         dv = dv + dot(probs_b, g, 0, 0)
+
+    stores = []
+
+    def store(src, dst):
+        copy = pltpu.make_async_copy(src, dst, lsem.at[8 + len(stores)])
+        copy.start()
+        stores.append(copy)
+
+    store(att_ref, att_out)
+    store(dq_ref, dq_out)
 
     stacked = jnp.concatenate([dk, dv], axis=1)
     dks[...] = stacked.reshape(4, 32, 2 * HD).astype(BF)
@@ -318,13 +384,15 @@
     reduce_y("w", weight_part, sh2, sw2, rh2, rw2, pass_on)
     turn(12, 16)
     opposite = zl * 8 + (y + 4) % 8
-    arrive(G.at[opposite, slice(0, 64)], "g+4")
-    arrive(G.at[opposite, slice(64, 128)], "g-4")
-    send(G.at[opposite], G.at[opposite], "gz4", twin)
+    for n, (rows, sign) in enumerate(zip(HALVES, "+-")):
+        arrive(G.at[opposite, rows], f"g{sign}4")
+        send(G.at[opposite, rows], G.at[opposite, rows], f"gz4{n}", twin)
     mine_cols = pl.ds(pl.multiple_of(zl * 128, 128), 128)
     twin_cols = pl.ds(pl.multiple_of((1 - zl) * 128, 128), 128)
     for j in range(2):
-        held[j] = settle_y("w", j, weight_part, rw2)
+        near = weight_part(j, y)
+        for n, rows in enumerate(HALVES):
+            held[j, rows, :] = settle_y("w", j, near[rows], rw2, n)
         zs[j] = held[j, :, twin_cols].astype(BF)
         send(zs.at[j], zr_.at[j], f"wz{j}", twin)
 
@@ -337,17 +405,36 @@
     for j in range(2):
         arrive(zr_.at[j], f"wz{j}")
         dkw_ref[j * 128 : j * 128 + 128, :] = (held[j, :, mine_cols] + zr_[j].astype(F32)).astype(BF)
+    store(dkw_ref, dkw_out)
     arrive(G_at(1, 0), "gz0")
     for k in (1, 2, 3):
         arrive(G_at(1, -k), f"gz+{k}")
         arrive(G_at(1, k), f"gz-{k}")
-    arrive(G_at(1, 4), "gz4")
+    for n, rows in enumerate(HALVES):
+        arrive(G.at[(1 - zl) * 8 + (y + 4) % 8, rows], f"gz4{n}")
     more_w, more_b = weight_grad(1 - zl)
     dw_ref[...] = (grad_w + more_w)[0:480].astype(BF)
     db_ref[...] = grad_b + more_b
+    store(dw_ref, dw_out)
+    store(db_ref, db_out)
     for copy in sends:
         copy.wait_send()
+    for copy in stores:
+        copy.wait()
     assert len(names.slots) <= SLOTS, len(names.slots)
+
+
+def write_out(*refs):
+    given, result, held, sem = refs[:5], refs[5:10], refs[10:15], refs[15]
+    load = [pltpu.make_async_copy(a, b, sem.at[i]) for i, (a, b) in enumerate(zip(given, held))]
+    save = [pltpu.make_async_copy(a, b, sem.at[5 + i]) for i, (a, b) in enumerate(zip(held, result))]
+    for copy in load:
+        copy.start()
+    for i in range(5):
+        load[i].wait()
+        save[i].start()
+    for copy in save:
+        copy.wait()
 
 
 def shards(
@@ -363,8 +450,8 @@
             jax.ShapeDtypeStruct((1, 256), F32),
             jax.ShapeDtypeStruct((256, 128), BF),
         ),
-        in_specs=[pl.BlockSpec(memory_space=vm)] * 8,
-        out_specs=[pl.BlockSpec(memory_space=vm)] * 5,
+        in_specs=[pl.BlockSpec(memory_space=pltpu.HBM)] * 8,
+        out_specs=[pl.BlockSpec(memory_space=pltpu.HBM)] * 5,
         scratch_shapes=[
             vm((32, 64, 512), BF),
             vm((512, 2048), BF),
@@ -396,17 +483,40 @@
             vm((3, 32, 256), BF),
             vm((32, 32, 256), BF),
             vm((16, 128, 256), BF),
+            vm((64, 480), BF),
+            vm((480, 256), BF),
+            vm((256,), BF),
+            vm((256, 2048), BF),
+            vm((256, 256), BF),
+            vm((256, 256), BF),
+            vm((1, 128), jnp.int32),
+            vm((1, 256), jnp.int32),
+            vm((256, 256), BF),
+            vm((256, 256), BF),
+            vm((480, 256), BF),
+            vm((1, 256), F32),
+            vm((256, 128), BF),
             pltpu.SemaphoreType.DMA((SLOTS,)),
             pltpu.SemaphoreType.DMA((SLOTS,)),
+            pltpu.SemaphoreType.DMA((13,)),
         ],
         compiler_params=pltpu.CompilerParams(
-            collective_id=0, has_side_effects=True, vmem_limit_bytes=48 * 2**20
+            collective_id=0, has_side_effects=True, vmem_limit_bytes=VMEM_ALL
         ),
         name="layer",
     )(
-        image_feats, proj_weight, proj_bias.reshape(1, 256), kv_weight, queries, out_grad,
-        image_sample, text_sample.reshape(256, 1),
+        image_feats, proj_weight, proj_bias, kv_weight, queries, out_grad,
+        image_sample, text_sample,
     )
+    out = pl.pallas_call(
+        write_out,
+        out_shape=[jax.ShapeDtypeStruct(a.shape, a.dtype) for a in out],
+        in_specs=[pl.BlockSpec(memory_space=pltpu.HBM)] * 5,
+        out_specs=[pl.BlockSpec(memory_space=pltpu.HBM)] * 5,
+        scratch_shapes=[vm(a.shape, a.dtype) for a in out] + [pltpu.SemaphoreType.DMA((10,))],
+        compiler_params=pltpu.CompilerParams(vmem_limit_bytes=VMEM_ALL),
+        name="results",
+    )(*out)
     attended, d_queries, d_proj, d_bias, d_kv = out
     return attended, d_queries, d_proj, d_bias.reshape(256), d_kv
 

time: 110 us -> 100 us (0.909)
  local copies, waits for them, and re-layouts: 8.62 us -> 0 us
    unnamed x17 -> x0, local copies, waits for them, and re-layouts: 7.11 us -> none
    pallas_call x1, Pallas kernels: 100 us -> 97.4 us  [shards(): pl.pallas_call(kernel, out_shape=(jax.ShapeDtypeStruct((256, 256), BF), j...]
    pallas_call x0 -> x1, Pallas kernels: none -> 1.87 us  [shards(): pl.pallas_call(write_out, out_shape=[jax.ShapeDtypeStruct(a.shape, a.dtyp...]
    reshape x2 -> x0, local copies, waits for them, and re-layouts: 1.51 us -> none  [the longest x1 0.82 us: shards(): text_sample.reshape(256, 1)]
where the time goes in v2:
time: 100 us; the launch traced here: 99.9 us
  Pallas kernels  99.3 us (99%)
    pallas_call x1, Pallas kernels, shards(): pl.pallas_call(kernel, out_shape=(jax.ShapeDtypeStruct((256, 256), BF), j...  97.4 us

profile of v2, /device:TPU:64, one launch (start us, length us, event | category | flops | bytes accessed | tf_op | source)
XLA Modules:
  0.0 99.9 jit_solution(18208190914369500178)
XLA Ops:
  0.6 97.4 %layer.1 = (bf16[256,256]{1,0:T(8,128)(2,1)}, bf16[256,256]{1,0:T(8,128)(2,1)}, bf16[480,256]{1,0:T(8,128)(2,1)}, f32[1,256]{1,0:T(1,128)}, bf16[256,128]{1,0:T(8,128)(2,1)}) custom-call(bf16[64,480]{1,0:T(8,128)(2,1)} %feat_in.1, bf16[480,256]{1,0:T(8,128)(2,1)} %w_in.1, bf16[256]{0:T(256)(128)(2,1)} %bias_in.1, bf16[256,2048]{1,0:T(8,128)(2,1)} %kvw_in.1, ...), custom_call_target="tpu_custom_call" | custom-call | tf_op jit(solution)/shard_map/layer/pallas_call | solution.py:444
  98.0 1.9 %results.1 = (bf16[256,256]{1,0:T(8,128)(2,1)}, bf16[256,256]{1,0:T(8,128)(2,1)}, bf16[480,256]{1,0:T(8,128)(2,1)}, f32[1,256]{1,0:T(1,128)}, bf16[256,128]{1,0:T(8,128)(2,1)}) custom-call(bf16[256,256]{1,0:T(8,128)(2,1)} %get-tuple-element.15.refs_0_, bf16[256,256]{1,0:T(8,128)(2,1)} %get-tuple-element.16.refs_1_, ...), custom_call_target="tpu_custom_call" | custom-call | tf_op jit(solution)/shard_map/results/pallas_call | solution.py:511

commit v3 on v2

--- a/solution.py
+++ b/solution.py
@@ -27,7 +27,6 @@
 
 SLOTS = 256
 VMEM_ALL = 67043328
-HALVES = (slice(0, 64), slice(64, 128))
 
 
 def kernel(
@@ -184,81 +183,91 @@
     last(3)
     last(1)
     last(2)
-    for h in range(KVH):
+
+    def reduce_y(tag, tile, s_half, s_whole, r_half, r_whole, between):
+        lanes = (slice(0, 128), slice(128, 256))
+        for n in range(2):
+            if n == 1:
+                between(0)
+            for j in range(2):
+                far = tile(j, (y + 4) % 8, n)
+                for d, way in enumerate((1, -1)):
+                    s_half[d, j, n] = far[:, lanes[d]].astype(BF)
+                    send(s_half.at[d, j, n], r_half.at[d, j, n], f"{tag}{d}{j}{n}0", ydev[way])
+        for k in (1, 2, 3):
+            between(k)
+            for j in range(2):
+                parts = [tile(j, (y + way * (4 - k) + 8) % 8, 2) for way in (1, -1)]
+                for n in range(2):
+                    for d, way in enumerate((1, -1)):
+                        part = parts[d][64 * n : 64 * n + 64]
+                        if k == 1:
+                            arrive(r_half.at[d, j, n], f"{tag}{d}{j}{n}0")
+                            halves = [part[:, lanes[0]], part[:, lanes[1]]]
+                            halves[d] = halves[d] + r_half[d, j, n].astype(F32)
+                            for l in range(2):
+                                s_whole[d, j, n, 0, :, lanes[l]] = halves[l].astype(BF)
+                        else:
+                            arrive(r_whole.at[d, j, n, k - 2], f"{tag}{d}{j}{n}{k - 1}")
+                            s_whole[d, j, n, k - 1] = (part + r_whole[d, j, n, k - 2].astype(F32)).astype(BF)
+                        source = s_whole.at[d, j, n, k - 1]
+                        send(source, r_whole.at[d, j, n, k - 1], f"{tag}{d}{j}{n}{k}", ydev[way])
+
+    def settle_y(tag, j, total, r_whole, n):
+        for d in range(2):
+            arrive(r_whole.at[d, j, n, 2], f"{tag}{d}{j}{n}3")
+            total = total + r_whole[d, j, n, 2].astype(F32)
+        return total
+
+    def partial(j, row, n):
+        shard = ((1 - zl if j == 0 else zl) * 8 + row) * 2
+        if n < 2:
+            return dot(F[shard + (c + n) % 2], W[...])
+        return dot(jnp.concatenate([F[shard + c], F[shard + 1 - c]], axis=0), W[...])
+
+    def meanwhile(k):
+        if k == 0:
+            for zr in range(4):
+                for xr in range(4):
+                    arrive(F.at[T(zr, xr, 1)], f"c{zr}{xr}")
+        if k == 1:
+            for h in range(KVH):
+                for half in range(2):
+                    cols = pl.ds(half * 1024 + h * HD, HD)
+                    KT[h, pl.ds(half * HD, HD), :] = kvw_ref[:, cols].T
+
+    reduce_y("p", partial, sh, sw, rh, rw, meanwhile)
+    both = partial(0, y, 2)
+    away = [both[:64], both[64:]]
+    both = partial(1, y, 2) + bias_ref[...].astype(F32).reshape(1, 256)
+    home = [both[:64], both[64:]]
+    for n in range(2):
+        zb[0, n] = settle_y("p", 0, away[n], rw, n).astype(BF)
+        send(zb.at[0, n], zb.at[1, n], f"pz{n}", twin)
+        home[n] = settle_y("p", 1, home[n], rw, n)
+    for n in range(2):
+        arrive(zb.at[1, n], f"pz{n}")
+        rows = pl.ds(pl.multiple_of((c + n) % 2 * 64, 64), 64)
+        proj[rows, :] = (home[n] + zb[1, n].astype(F32)).astype(BF)
+    projected = proj[...]
+
+    for zr in (2, 1, 3, 0):
+        zq = (zh + zr) % 4
         for half in range(2):
-            cols = pl.ds(half * 1024 + h * HD, HD)
-            KT[h, pl.ds(half * HD, HD), :] = kvw_ref[:, cols].T
-    for zr in range(4):
-        for xr in range(4):
-            arrive(F.at[T(zr, xr, 1)], f"c{zr}{xr}")
-
-    def reduce_y(tag, tile, s_half, s_whole, r_half, r_whole, between=None):
-        lanes = (slice(0, 128), slice(128, 256))
-        for j in range(2):
-            far = tile(j, (y + 4) % 8)
-            for n, rows in enumerate(HALVES):
-                for d, way in enumerate((1, -1)):
-                    s_half[d, j, rows, :] = far[rows, lanes[d]].astype(BF)
-                    send(s_half.at[d, j, rows], r_half.at[d, j, rows], f"{tag}{d}{j}{n}0", ydev[way])
-        for k in (1, 2, 3):
-            if between is not None:
-                between(k)
-            for j in range(2):
-                parts = [tile(j, (y + way * (4 - k) + 8) % 8) for way in (1, -1)]
-                for n, rows in enumerate(HALVES):
-                    for d, way in enumerate((1, -1)):
-                        part = parts[d][rows]
-                        if k == 1:
-                            arrive(r_half.at[d, j, rows], f"{tag}{d}{j}{n}0")
-                            halves = [part[:, lanes[0]], part[:, lanes[1]]]
-                            halves[d] = halves[d] + r_half[d, j, rows, :].astype(F32)
-                            for l in range(2):
-                                s_whole[d, j, 0, rows, lanes[l]] = halves[l].astype(BF)
-                        else:
-                            got = r_whole.at[d, j, k - 2, rows]
-                            arrive(got, f"{tag}{d}{j}{n}{k - 1}")
-                            s_whole[d, j, k - 1, rows, :] = (part + got[...].astype(F32)).astype(BF)
-                        source = s_whole.at[d, j, k - 1, rows]
-                        send(source, r_whole.at[d, j, k - 1, rows], f"{tag}{d}{j}{n}{k}", ydev[way])
-
-    def settle_y(tag, j, tile, r_whole, n):
-        for d in range(2):
-            got = r_whole.at[d, j, 2, HALVES[n]]
-            arrive(got, f"{tag}{d}{j}{n}3")
-            tile = tile + got[...].astype(F32)
-        return tile
-
-    def partial(j, row):
-        shard = ((1 - zl if j == 0 else zl) * 8 + row) * 2
-        rows = F[pl.ds(shard, 2)].reshape(128, 512)
-        return dot(rows, W[...])
-
-    reduce_y("p", partial, sh, sw, rh, rw)
-    away = partial(0, y)
-    home = partial(1, y) + bias_ref[...].astype(F32).reshape(1, 256)
-    for n, rows in enumerate(HALVES):
-        zb[0, rows, :] = settle_y("p", 0, away[rows], rw, n).astype(BF)
-        send(zb.at[0, rows], zb.at[1, rows], f"pz{n}", twin)
-    settled = [settle_y("p", 1, home[rows], rw, n) for n, rows in enumerate(HALVES)]
-    for n, rows in enumerate(HALVES):
-        arrive(zb.at[1, rows], f"pz{n}")
-        settled[n] = settled[n] + zb[1, rows, :].astype(F32)
-    projected = jnp.concatenate(settled, axis=0).astype(BF)
-    proj[...] = projected
-
-    for h in range(KVH):
-        for half in range(2):
-            cols = pl.ds(half * 1024 + h * HD, HD)
+            cols = pl.ds(pl.multiple_of(half * 1024 + zq * 256, 256), 256)
             block = dot(projected, kvw_ref[:, cols]).astype(BF)
-            for m in range(4):
-                kvp[m % 2, (h % 2) * 2 + m // 2, h // 2, :, pl.ds(half * HD, HD)] = block[32 * m : 32 * m + 32]
-    send(kvp.at[1 - c], kvr, "kc", core)
+            for h in range(2):
+                for m in range(4):
+                    kvp[m // 2, zr, h * 2 + m % 2, :, pl.ds(half * HD, HD)] = block[
+                        32 * m : 32 * m + 32, h * HD : h * HD + HD
+                    ]
+        send(kvp.at[1 - c, zr], kvr.at[zr], f"kc{zr}", core)
+    for zr in (2, 1, 3, 0):
+        arrive(kvr.at[zr], f"kc{zr}")
+        sx[zr] = (kvp[c, zr].astype(F32) + kvr[zr].astype(F32)).astype(BF)
+        for r in (2, 1, 3):
+            send(sx.at[zr, (x + r) % 4], rx.at[r - 1, zr], f"kx{r}{zr}", xdev[r])
     projT[...] = projected.T
-    arrive(kvr, "kc")
-    sx[...] = (kvp[c].astype(F32) + kvr[...].astype(F32)).astype(BF)
-    for zr in (2, 1, 3, 0):
-        for r in (2, 1, 3):
-            send(sx.at[(x + r) % 4, (zh + zr) % 4], rx.at[r - 1, zr], f"kx{r}{zr}", xdev[r])
 
     def turn(lo, hi):
         def body(s, carry):
@@ -270,7 +279,7 @@
 
     turn(0, 4)
     for zr in (2, 1, 3, 0):
-        acc = sx[x, (zh + zr) % 4].astype(F32)
+        acc = sx[zr, x].astype(F32)
         for r in (1, 3, 2):
             arrive(rx.at[r - 1, zr], f"kx{r}{zr}")
             acc = acc + rx[r - 1, zr].astype(F32)
@@ -281,13 +290,13 @@
     for r in (1, 3, 2):
         arrive(rz.at[r - 1], f"kz{r}")
         acc = acc + rz[r - 1].astype(F32)
-    m = (x % 2) * 2 + c
+    m = c * 2 + x % 2
     kvg[m] = acc.astype(BF)
     for f, dev in enumerate(flips):
         send(kvg.at[m], kvg.at[m], f"kg{f}", dev)
     texts = jnp.broadcast_to(txt_ref[...].astype(F32), (HD, 256)).T
     allowed = texts == img_ref[...].astype(F32)
-    mates = ((x % 2) * 2 + 1 - c, (1 - x % 2) * 2 + c, (1 - x % 2) * 2 + 1 - c)
+    mates = (2 - 2 * c + x % 2, 2 * c + 1 - x % 2, 2 - 2 * c + 1 - x % 2)
     for f in range(3):
         arrive(kvg.at[mates[f]], f"kg{f}")
     both = kvg[...].reshape(HD, 2 * HD)
@@ -329,8 +338,13 @@
     for f in range(3):
         arrive(dkr.at[f], f"dk{f}")
         mine = mine + dkr[f].astype(F32)
-    D[t] = mine.astype(BF)
-    own_d = D.at[t]
+
+    def D_at(zr, xr, cr=0):
+        xq = (x + xr) % 4
+        return D.at[(((zh + zr) % 4 * 2 + xq // 2) * 2 + (c + cr) % 2) * 2 + xq % 2]
+
+    own_d = D_at(0, 0)
+    own_d[...] = mine.astype(BF)
     for r in (2, 1, 3):
         send(own_d, own_d, f"dz{r}", zdev[r])
     for r in (2, 1, 3):
@@ -338,63 +352,66 @@
     send(own_d, own_d, "dc00", core)
     turn(8, 12)
     for r in (1, 3, 2):
-        ref = D.at[T(4 - r)]
+        ref = D_at(4 - r, 0)
         arrive(ref, f"dz{r}")
         for s in (2, 1, 3):
             send(ref, ref, f"dx{4 - r}{s}", xdev[s])
         send(ref, ref, f"dc{4 - r}0", core)
     for zr in (0, 3, 1, 2):
         for s in (1, 3, 2):
-            ref = D.at[T(zr, 4 - s)]
+            ref = D_at(zr, 4 - s)
             arrive(ref, f"dx{zr}{s}")
             send(ref, ref, f"dc{zr}{4 - s}", core)
-    for zr in range(4):
-        for xr in range(4):
-            arrive(D.at[T(zr, xr, 1)], f"dc{zr}{xr}")
-
-    grad = jnp.zeros((128, 256), F32)
-    for h in range(KVH):
-        grad = grad + dot(D[4 * h : 4 * h + 4].reshape(128, 256), KT[h])
-
-    def G_at(zr, yr):
+
+    def G_at(zr, yr, n):
         side = zl if zr == 0 else 1 - zl
-        return G.at[side * 8 + (y + yr + 8) % 8]
-
-    G[zl * 8 + y] = grad.astype(BF)
-    piece = G_at(0, 0)
-    send(piece, piece, "g+1", ydev[1])
-    send(piece, piece, "g-1", ydev[-1])
-    send(piece, piece, "gz0", twin)
-
-    def weight_part(j, row):
+        return G.at[side * 8 + (y + yr + 8) % 8, (c + n) % 2]
+
+    for n in range(2):
+        if n == 1:
+            for zr in range(4):
+                for xr in range(4):
+                    arrive(D_at(zr, xr, 1), f"dc{zr}{xr}")
+        grad = jnp.zeros((64, 256), F32)
+        for h in range(KVH):
+            rows = D[pl.ds(4 * h + (c + n) % 2 * 2, 2)].reshape(64, 256)
+            grad = grad + dot(rows, KT[h])
+        piece = G_at(0, 0, n)
+        piece[...] = grad.astype(BF)
+        send(piece, piece, f"g+1{n}", ydev[1])
+        send(piece, piece, f"g-1{n}", ydev[-1])
+        send(piece, piece, f"gz0{n}", twin)
+
+    def weight_part(j, row, n):
         rows = D[pl.ds(row * 4, 4)].reshape(128, 256)
-        return dot(projT[j * 128 : j * 128 + 128, :], rows)
+        top = j * 128 + n % 2 * 64
+        return dot(projT[top : top + (64 if n < 2 else 128), :], rows)
 
     def pass_on(k):
-        for way, sign, rows in ((1, "+", slice(0, 64)), (-1, "-", slice(64, 128))):
-            piece = G_at(0, -way * k)
-            arrive(piece, f"g{sign}{k}")
-            if k < 3:
-                send(piece, piece, f"g{sign}{k + 1}", ydev[way])
-            else:
-                index = zl * 8 + (y - way * k + 8) % 8
-                send(G.at[index, rows], G.at[index, rows], f"g{sign}4", ydev[way])
-            send(piece, piece, f"gz{sign}{k}", twin)
+        if k == 0:
+            return
+        for n in range(2):
+            for d, (way, sign) in enumerate(((1, "+"), (-1, "-"))):
+                piece = G_at(0, -way * k, n)
+                arrive(piece, f"g{sign}{k}{n}")
+                if k < 3 or n == d:
+                    send(piece, piece, f"g{sign}{k + 1}{n}", ydev[way])
+                send(piece, piece, f"gz{sign}{k}{n}", twin)
 
     reduce_y("w", weight_part, sh2, sw2, rh2, rw2, pass_on)
     turn(12, 16)
-    opposite = zl * 8 + (y + 4) % 8
-    for n, (rows, sign) in enumerate(zip(HALVES, "+-")):
-        arrive(G.at[opposite, rows], f"g{sign}4")
-        send(G.at[opposite, rows], G.at[opposite, rows], f"gz4{n}", twin)
+    for n, sign in enumerate("+-"):
+        piece = G_at(0, 4, n)
+        arrive(piece, f"g{sign}4{n}")
+        send(piece, piece, f"gz4{n}", twin)
     mine_cols = pl.ds(pl.multiple_of(zl * 128, 128), 128)
     twin_cols = pl.ds(pl.multiple_of((1 - zl) * 128, 128), 128)
     for j in range(2):
-        near = weight_part(j, y)
-        for n, rows in enumerate(HALVES):
-            held[j, rows, :] = settle_y("w", j, near[rows], rw2, n)
-        zs[j] = held[j, :, twin_cols].astype(BF)
-        send(zs.at[j], zr_.at[j], f"wz{j}", twin)
+        near = weight_part(j, y, 2)
+        for n in range(2):
+            held[j, n] = settle_y("w", j, near[64 * n : 64 * n + 64], rw2, n)
+            zs[j, n] = held[j, n, :, twin_cols].astype(BF)
+            send(zs.at[j, n], zr_.at[j, n], f"wz{j}{n}", twin)
 
     def weight_grad(side):
         rows = G[pl.ds(side * 8, 8)].reshape(1024, 256)
@@ -403,15 +420,17 @@
 
     grad_w, grad_b = weight_grad(zl)
     for j in range(2):
-        arrive(zr_.at[j], f"wz{j}")
-        dkw_ref[j * 128 : j * 128 + 128, :] = (held[j, :, mine_cols] + zr_[j].astype(F32)).astype(BF)
+        for n in range(2):
+            arrive(zr_.at[j, n], f"wz{j}{n}")
+            top = j * 128 + n * 64
+            dkw_ref[top : top + 64, :] = (held[j, n, :, mine_cols] + zr_[j, n].astype(F32)).astype(BF)
     store(dkw_ref, dkw_out)
-    arrive(G_at(1, 0), "gz0")
-    for k in (1, 2, 3):
-        arrive(G_at(1, -k), f"gz+{k}")
-        arrive(G_at(1, k), f"gz-{k}")
-    for n, rows in enumerate(HALVES):
-        arrive(G.at[(1 - zl) * 8 + (y + 4) % 8, rows], f"gz4{n}")
+    for n in range(2):
+        arrive(G_at(1, 0, n), f"gz0{n}")
+        for k in (1, 2, 3):
+            arrive(G_at(1, -k, n), f"gz+{k}{n}")
+            arrive(G_at(1, k, n), f"gz-{k}{n}")
+        arrive(G_at(1, 4, n), f"gz4{n}")
     more_w, more_b = weight_grad(1 - zl)
     dw_ref[...] = (grad_w + more_w)[0:480].astype(BF)
     db_ref[...] = grad_b + more_b
@@ -458,20 +477,20 @@
             vm((512, 256), BF),
             vm((64, 512), BF),
             vm((KVH, 256, 256), BF),
-            vm((2, 2, 128, 128), BF),
-            vm((2, 2, 3, 128, 256), BF),
-            vm((2, 2, 128, 128), BF),
-            vm((2, 2, 3, 128, 256), BF),
-            vm((2, 128, 256), BF),
+            vm((2, 2, 2, 64, 128), BF),
+            vm((2, 2, 2, 3, 64, 256), BF),
+            vm((2, 2, 2, 64, 128), BF),
+            vm((2, 2, 2, 3, 64, 256), BF),
+            vm((2, 2, 64, 256), BF),
             vm((128, 256), BF),
             vm((256, 128), BF),
-            vm((2, 2, 128, 128), BF),
-            vm((2, 2, 3, 128, 256), BF),
-            vm((2, 2, 128, 128), BF),
-            vm((2, 2, 3, 128, 256), BF),
-            vm((2, 128, 256), F32),
-            vm((2, 128, 128), BF),
-            vm((2, 128, 128), BF),
+            vm((2, 2, 2, 64, 128), BF),
+            vm((2, 2, 2, 3, 64, 256), BF),
+            vm((2, 2, 2, 64, 128), BF),
+            vm((2, 2, 2, 3, 64, 256), BF),
+            vm((2, 2, 64, 256), F32),
+            vm((2, 2, 64, 128), BF),
+            vm((2, 2, 64, 128), BF),
             vm((2, 4, 4, 32, 256), BF),
             vm((4, 4, 32, 256), BF),
             vm((4, 4, 32, 256), BF),
@@ -482,7 +501,7 @@
             vm((4, 32, 256), BF),
             vm((3, 32, 256), BF),
             vm((32, 32, 256), BF),
-            vm((16, 128, 256), BF),
+            vm((16, 2, 64, 256), BF),
             vm((64, 480), BF),
             vm((480, 256), BF),
             vm((256,), BF),

time: 100 us -> 99.9 us (level)
  no operation moved by 1% of the time
where the time goes in v3:
time: 99.9 us; the launch traced here: 99.7 us
  Pallas kernels  99.1 us (99%)
    pallas_call x1, Pallas kernels, shards(): pl.pallas_call(kernel, out_shape=(jax.ShapeDtypeStruct((256, 256), BF), j...  97.2 us

profile of v3, /device:TPU:64, one launch (start us, length us, event | category | flops | bytes accessed | tf_op | source)
XLA Modules:
  0.0 99.7 jit_solution(18259636565250052150)
XLA Ops:
  0.6 97.2 %layer.1 = (bf16[256,256]{1,0:T(8,128)(2,1)}, bf16[256,256]{1,0:T(8,128)(2,1)}, bf16[480,256]{1,0:T(8,128)(2,1)}, f32[1,256]{1,0:T(1,128)}, bf16[256,128]{1,0:T(8,128)(2,1)}) custom-call(bf16[64,480]{1,0:T(8,128)(2,1)} %feat_in.1, bf16[480,256]{1,0:T(8,128)(2,1)} %w_in.1, bf16[256]{0:T(256)(128)(2,1)} %bias_in.1, bf16[256,2048]{1,0:T(8,128)(2,1)} %kvw_in.1, ...), custom_call_target="tpu_custom_call" | custom-call | tf_op jit(solution)/shard_map/layer/pallas_call | solution.py:463
  97.9 1.9 %results.1 = (bf16[256,256]{1,0:T(8,128)(2,1)}, bf16[256,256]{1,0:T(8,128)(2,1)}, bf16[480,256]{1,0:T(8,128)(2,1)}, f32[1,256]{1,0:T(1,128)}, bf16[256,128]{1,0:T(8,128)(2,1)}) custom-call(bf16[256,256]{1,0:T(8,128)(2,1)} %get-tuple-element.15.refs_0_, bf16[256,256]{1,0:T(8,128)(2,1)} %get-tuple-element.16.refs_1_, ...), custom_call_target="tpu_custom_call" | custom-call | tf_op jit(solution)/shard_map/results/pallas_call | solution.py:530
